TPU v7x, 256 devices: a whole 4x4x8 slice. The times are simulated.
256 devices in a mesh: dp: 8 (over z_lo, core), expert: 32 (over y, x, z_hi).
Axes of the slice: x: 4, y: 4, z: 8 (z_hi: 2, z_lo: 4; z = z_hi * 4 + z_lo), core: 2. Of those that a mesh axis runs over, the one named last changes fastest.
Arguments:
- tokens: bfloat16 [32768, 3584], P(('dp', 'expert')), may hold values from -6 to 6
- cotangent: bfloat16 [32768, 3584], P(('dp', 'expert')), may hold values from -6 to 6
- gates: float32 [32768, 1], P(('dp', 'expert')), may hold values from 0.1 to 1
- routes: int32 [32768, 1], P(('dp', 'expert')), may hold values from 0 to 31; in each aligned block of 128 rows (0 to 127, 128 to 255, ...) at most 5 rows name the same one
- w_up: bfloat16 [32, 3584, 1024], P('expert', None, 'dp'), may hold values from -0.09375 to 0.09375
- w_down: bfloat16 [32, 1024, 3584], P('expert', 'dp'), may hold values from -0.1875 to 0.1875
- m_up: bfloat16 [32, 3584, 1024], P('expert', None, 'dp'), may hold values from -3 to 3
- v_up: bfloat16 [32, 3584, 1024], P('expert', None, 'dp'), may hold values from 0.099609375 to 1
- m_down: bfloat16 [32, 1024, 3584], P('expert', 'dp'), may hold values from -3 to 3
- v_down: bfloat16 [32, 1024, 3584], P('expert', 'dp'), may hold values from 0.099609375 to 1
- leaving: int32 [1], replicated, may hold values from 0 to 31
- tile_owner: int32 [32], replicated, may hold values from 0 to 31, each once
Outputs:
- update_up: bfloat16 [32, 3584, 1024], P('expert', None, 'dp')
- update_down: bfloat16 [32, 1024, 3584], P('expert', 'dp')
- adopted_up: bfloat16 [32, 112, 1024], P('expert', None, 'dp')
- adopted_down: bfloat16 [32, 112, 1024], P('expert', None, 'dp')
Inputs may be any that keep to these rules, and one draw needn't show every extreme that they name: `routes`: each row names one expert; within the 128 rows of one device no expert is named more than 5 times, a bound that some block reaches in some devices. `tile_owner`: A permutation of the 32 device indices of the expert axis.
All inputs are finite; a program needn't handle non-finite values.
Results may differ from a plain program's by a relative error of at most 0.0041.
Values may be sent and summed in bfloat16 or wider, within the bound.
A program may use at most 128 MiB of HBM per device.

v0:
```python
import jax
import jax.numpy as jnp
from jax import lax
from jax.sharding import PartitionSpec as P

BETA_ONE = 0.9
BETA_TWO = 0.95
EPSILON = 1e-08


def expert_terms(rows_x, rows_c, up_tile, down_tile):
    preact = jnp.dot(rows_x, up_tile, preferred_element_type=jnp.float32)
    squash = jax.nn.sigmoid(preact)
    hidden = (preact * squash).astype(jnp.bfloat16)
    slope_val = squash * (1.0 + preact * (1.0 - squash))
    back_grad = lax.dot_general(
        rows_c, down_tile, (((1,), (1,)), ((), ())), preferred_element_type=jnp.float32
    )
    pre_grad = (back_grad * slope_val).astype(jnp.bfloat16)
    grad_up = lax.dot_general(
        rows_x, pre_grad, (((0,), (0,)), ((), ())), preferred_element_type=jnp.float32
    )
    grad_cols = lax.dot_general(
        rows_c, hidden, (((0,), (0,)), ((), ())), preferred_element_type=jnp.float32
    )
    return (grad_up, grad_cols)


def adam_step(gradient, moment_one, moment_two):
    new_one = BETA_ONE * moment_one.astype(jnp.float32) + (1.0 - BETA_ONE) * gradient
    new_two = BETA_TWO * moment_two.astype(jnp.float32) + (1.0 - BETA_TWO) * gradient * gradient
    return (new_one / (jnp.sqrt(new_two) + EPSILON)).astype(jnp.bfloat16)


def on_device(
    tokens, cotangent, gates, routes, w_up, w_down, m_up, v_up, m_down, v_down, leaving, tile_owner
):
    experts = lax.axis_size("expert")
    my_index = lax.axis_index("expert")
    tok_count, model_width = tokens.shape
    top_count = routes.shape[1]
    hidden_units = w_up.shape[2]
    capacity = 5 * tok_count * top_count // (4 * experts)
    pair_count = tok_count * top_count
    leaver = leaving[0]
    slot_ids = jnp.arange(experts, dtype=jnp.int32)
    tile_rows = model_width // experts
    adopt = jnp.sum(
        jnp.where(tile_owner[None, :] == slot_ids[:, None], slot_ids[None, :], 0), axis=1
    )
    expert_of = routes.reshape(pair_count)
    member = (expert_of[:, None] == slot_ids[None, :]).astype(jnp.int32)
    slot_rank = jnp.sum((jnp.cumsum(member, axis=0) - 1) * member, axis=1)
    slot_place = expert_of * capacity + slot_rank
    staying = expert_of != leaver
    send_mask = jnp.ones_like(staying)
    pair_x = jnp.repeat(tokens, top_count, axis=0)
    pair_c = (
        gates.reshape(pair_count)[:, None]
        * jnp.repeat(cotangent, top_count, axis=0).astype(jnp.float32)
    ).astype(jnp.bfloat16)
    pair_both = jnp.concatenate([pair_x, pair_c], axis=1)
    targets = jnp.arange(experts * capacity, dtype=jnp.int32)
    picker = ((slot_place[None, :] == targets[:, None]) & send_mask[None, :]).astype(jnp.bfloat16)
    send_both = jnp.dot(picker, pair_both, preferred_element_type=jnp.float32).astype(jnp.bfloat16)
    send_x = send_both[:, :model_width].reshape(experts, capacity, model_width)
    send_c = send_both[:, model_width:].reshape(experts, capacity, model_width)
    recv_x, recv_c = (
        lax.all_to_all(send_x, "expert", split_axis=0, concat_axis=0, tiled=True),
        lax.all_to_all(send_c, "expert", split_axis=0, concat_axis=0, tiled=True),
    )
    recv_x = recv_x.reshape(experts * capacity, model_width)
    recv_c = recv_c.reshape(experts * capacity, model_width)
    grad_up, grad_cols = expert_terms(
        lax.all_gather(recv_x, "dp", axis=0, tiled=True),
        lax.all_gather(recv_c, "dp", axis=0, tiled=True),
        w_up[0],
        w_down[0],
    )
    keep_own = my_index != leaver
    step_up = adam_step(grad_up, m_up[0], v_up[0])
    step_down = adam_step(grad_cols.T, m_down[0], v_down[0])
    both_steps = jnp.concatenate([step_up, step_down.T], axis=1).reshape(
        experts, tile_rows, 2 * hidden_units
    )
    ordered = both_steps[adopt]
    outgoing = jnp.where(keep_own, jnp.zeros_like(ordered), ordered)
    incoming = lax.all_to_all(outgoing, "expert", split_axis=0, concat_axis=0, tiled=True)
    mine = lax.dynamic_index_in_dim(incoming, leaver, 0, keepdims=False)
    adopted_up = mine[:, :hidden_units][None]
    adopted_down = mine[:, hidden_units:][None]
    update_up = jnp.where(keep_own, step_up, jnp.zeros_like(step_up))[None]
    update_down = jnp.where(keep_own, step_down, jnp.zeros_like(step_down))[None]
    return (update_up, update_down, adopted_up, adopted_down)


def solution(mesh):
    placed = (
        P(("dp", "expert"), None),
        P(("dp", "expert"), None),
        P(("dp", "expert"), None),
        P(("dp", "expert"), None),
        P("expert", None, "dp"),
        P("expert", "dp", None),
        P("expert", None, "dp"),
        P("expert", None, "dp"),
        P("expert", "dp", None),
        P("expert", "dp", None),
        P(),
        P(),
    )
    return jax.shard_map(
        on_device,
        mesh=mesh,
        in_specs=placed,
        out_specs=(
            P("expert", None, "dp"),
            P("expert", "dp", None),
            P("expert", None, "dp"),
            P("expert", None, "dp"),
        ),
        check_vma=False,
    )
```

profile of v0, /device:TPU:33, one launch (start us, length us, event | category | flops | bytes accessed | tf_op | source)
XLA Modules:
  0.0 402.2 jit_solution(538637933655754063)
XLA Ops:
  7.2 0.0 copy-start
  7.2 0.0 copy-start.7
  7.2 0.0 all-gather.3.cloned.1.call-start
  7.2 0.9 fusion.19
  8.1 0.2 reduce_window_sum.11
  8.3 0.8 select_reduce_fusion
  9.1 0.7 multiply_add_fusion
  9.8 1.4 multiply_convert_fusion
  11.2 0.0 copy-done.7
  11.2 0.7 convolution_convert_fusion
  11.9 1.5 fusion.25
  13.5 1.5 reshape.61
  15.0 61.8 %all_to_all.15 = bf16[32,5,3584]{2,1,0:T(8,128)(2,1)} all-to-all(bf16[32,5,3584]{2,1,0:T(8,128)(2,1)S(1)} %reshape.61), channel_id=1, replica_groups=mesh['dp'=8,'expert'=32] {'expert'}, dimensions={0} | all-to-all | bytes 2293760 | tf_op jit(solution)/shard_map/all_to_all | solution.py:69
  76.8 2.5 reshape.62
  79.3 0.0 all-gather.3.cloned.1.call-update
  79.3 0.0 all-gather.5.cloned.1.call-start
  79.4 1.5 reshape.63
  80.9 62.4 %all_to_all.16 = bf16[32,5,3584]{2,1,0:T(8,128)(2,1)} all-to-all(bf16[32,5,3584]{2,1,0:T(8,128)(2,1)S(1)} %reshape.63), channel_id=1, replica_groups=mesh['dp'=8,'expert'=32] {'expert'}, dimensions={0} | all-to-all | bytes 2293760 | tf_op jit(solution)/shard_map/all_to_all | solution.py:70
  143.4 2.6 reshape.64
  146.0 0.0 all-gather.5.cloned.1.call-update
  146.7 0.0 copy-done.2
  146.7 0.0 copy-start.9
  146.7 1.3 copy.24
  148.0 0.0 copy-done.3
  148.0 1.3 copy.25
  149.3 0.0 copy-done.9
  149.3 0.1 select_reduce_fusion.1
  149.4 52.1 %all-gather.3.cloned.1.call-done = bf16[1280,3584]{1,0:T(8,128)(2,1)} async-done(((bf16[160,3584]{1,0:T(8,128)(2,1)}), bf16[1280,3584]{1,0:T(8,128)(2,1)}) %all-gather.3.cloned.1.call-update) | async-done | bytes 9175056 | tf_op jit(solution)/shard_map/all_gather | solution.py:75
  201.5 0.0 copy-done.8
  201.5 6.2 %fusion.14 = f32[1280,128]{1,0:T(8,128)S(1)} fusion(bf16[1280,3584]{1,0:T(8,128)(2,1)} %all-gather.3.cloned.1.call-done, bf16[1,3584,128]{2,1,0:T(8,128)(2,1)S(1)} %copy-done.8), kind=kOutput, calls=%fused_computation.24 | convolution fusion | flops 1174405120 | bytes 10747904 | tf_op jit(solution)/shard_map/dot_general | solution.py:12
  207.7 0.0 copy-start.5
  207.7 0.0 copy-start.6
  207.7 96.3 %all-gather.5.cloned.1.call-done = bf16[1280,3584]{1,0:T(8,128)(2,1)} async-done(((bf16[160,3584]{1,0:T(8,128)(2,1)}), bf16[1280,3584]{1,0:T(8,128)(2,1)}) %all-gather.5.cloned.1.call-update) | async-done | bytes 9175056 | tf_op jit(solution)/shard_map/all_gather | solution.py:76
  304.0 7.4 %fusion.12 = bf16[128,3584]{1,0:T(8,128)(2,1)} fusion(bf16[1,128,3584]{2,1,0:T(8,128)(2,1)} %param.21, bf16[1,128,3584]{2,1,0:T(8,128)(2,1)} %param.20, bf16[1280,3584]{1,0:T(8,128)(2,1)} %all-gather.5.cloned.1.call-done, f32[1280,128]{1,0:T(8,128)S(1)} %fusion.14), kind=kOutput, calls=%fused_computation.21 | convolution fusion | flops 1180729344 | bytes 12582912 | tf_op jit(solution)/shard_map/dot_general | solution.py:23
  311.4 0.0 copy-done
  311.4 0.0 copy-done.5
  311.4 0.0 copy-done.6
  311.4 14.3 %select_bitcast_fusion.1 = (bf16[1,3584,128]{1,2,0:T(8,128)(2,1)}, bf16[3584,128]{0,1:T(8,128)(2,1)}) fusion(pred[]{:T(512)S(6)} %ne.3, bf16[1,3584,128]{1,2,0:T(8,128)(2,1)S(1)} %copy-done.6, bf16[1,3584,128]{1,2,0:T(8,128)(2,1)S(1)} %copy-done.5, bf16[1280,3584]{1,0:T(8,128)(2,1)} %all-gather.3.cloned.1.call-done, ...), kind=kOutput, calls=%fused_computation.28 | convolution fusion | flops 2356248576 | bytes 23592960 | tf_op jit(solution)/shard_map/dot_general | solution.py:20
  325.7 1.6 pad_maximum_fusion
  327.3 2.3 copy.26
  329.6 2.2 gather_fusion
  331.7 1.4 broadcast_select_fusion
  333.1 10.5 %all-to-all-start.2 = ((bf16[32,112,256]{2,1,0:T(8,128)(2,1)}), bf16[32,112,256]{2,1,0:T(8,128)(2,1)}, u32[]{:S(2)}, u32[]{:S(2)}) async-start(bf16[32,112,256]{2,1,0:T(8,128)(2,1)} %broadcast_select_fusion), calls=%async_computation.2 | async-start | bytes 3670016 | tf_op jit(solution)/shard_map/all_to_all | solution.py:88
  343.6 1.3 copy.27
  344.9 1.0 select_bitcast_fusion
  345.9 48.0 %all-to-all-done.2 = bf16[32,112,256]{2,1,0:T(8,128)(2,1)} async-done(((bf16[32,112,256]{2,1,0:T(8,128)(2,1)}), bf16[32,112,256]{2,1,0:T(8,128)(2,1)}, u32[]{:S(2)}, u32[]{:S(2)}) %all-to-all-start.2) | async-done | bytes 1835040 | tf_op jit(solution)/shard_map/all_to_all | solution.py:88
  393.9 0.8 dynamic-slice_bitcast_fusion
  394.7 0.6 slice_bitcast_fusion
  (9 shorter events, 0.0 us)
Async XLA Ops:
  7.2 304.2 %copy-start = (bf16[1,128,3584]{2,1,0:T(8,128)(2,1)S(1)}, bf16[1,128,3584]{2,1,0:T(8,128)(2,1)}, u32[]{:S(2)}) copy-start(bf16[1,128,3584]{2,1,0:T(8,128)(2,1)} %param.17) | copy-start | bytes 2752516
  7.2 4.0 copy-start.7
  7.2 194.3 %all-gather.3.cloned.1.call-start = ((), (), s32[]{:S(2)}) async-start(), calls=%async_computation.3 | async-start | bytes 10321920 | tf_op jit(solution)/shard_map/all_gather | solution.py:75
  79.3 224.6 %all-gather.5.cloned.1.call-start = ((), (), s32[]{:S(2)}) async-start(), calls=%async_computation.4 | async-start | bytes 10321920 | tf_op jit(solution)/shard_map/all_gather | solution.py:76
  143.3 3.4 copy-start.2
  146.0 2.1 copy-start.3
  146.7 2.6 copy-start.9
  148.0 53.5 %copy-start.8 = (bf16[1,3584,128]{2,1,0:T(8,128)(2,1)S(1)}, bf16[1,3584,128]{2,1,0:T(8,128)(2,1)}, u32[]{:S(2)}) copy-start(bf16[1,3584,128]{2,1,0:T(8,128)(2,1)} %param.16) | copy-start | bytes 2752516
  207.7 103.7 %copy-start.5 = (bf16[1,3584,128]{1,2,0:T(8,128)(2,1)S(1)}, bf16[1,3584,128]{1,2,0:T(8,128)(2,1)}, u32[]{:S(2)}) copy-start(bf16[1,3584,128]{1,2,0:T(8,128)(2,1)} %copy.24) | copy-start | bytes 2752516
  207.7 103.7 %copy-start.6 = (bf16[1,3584,128]{1,2,0:T(8,128)(2,1)S(1)}, bf16[1,3584,128]{1,2,0:T(8,128)(2,1)}, u32[]{:S(2)}) copy-start(bf16[1,3584,128]{1,2,0:T(8,128)(2,1)} %copy.25) | copy-start | bytes 2752516
  333.1 10.5 %copy-start.4 = (bf16[1,3584,128]{1,2,0:T(8,128)(2,1)S(1)}, bf16[1,3584,128]{1,2,0:T(8,128)(2,1)}, u32[]{:S(2)}) copy-start(bf16[1,3584,128]{1,2,0:T(8,128)(2,1)} %get-tuple-element.16) | copy-start | bytes 2752516
  333.1 60.8 %all-to-all-start.2 = ((bf16[32,112,256]{2,1,0:T(8,128)(2,1)}), bf16[32,112,256]{2,1,0:T(8,128)(2,1)}, u32[]{:S(2)}, u32[]{:S(2)}) async-start(bf16[32,112,256]{2,1,0:T(8,128)(2,1)} %broadcast_select_fusion), calls=%async_computation.2 | async-start | bytes 3670016 | tf_op jit(solution)/shard_map/all_to_all | solution.py:88
  343.6 1.3 copy-start.1
Sparse Core Ops, SparseCore 0:
  79.5 122.0 all-gather.2
  203.3 100.6 all-gather.4
where the time goes:
time: 403 us; the launch traced here: 402 us
  waiting for transfers between devices  196 us (49%)
  blocking collectives  124 us (31%)
  matrix products  28.6 us (7%)
  local copies, waits for them, and re-layouts  19.5 us (5%)
  between operations  14.9 us (4%)
  starting transfers between devices  10.6 us (3%)
  other arithmetic  7.97 us (2%)
    all_gather x1, waiting for transfers between devices, on_device(): lax.all_gather(recv_c, 'dp', axis=0, tiled=True)  96.3 us
    all_to_all x1, blocking collectives, on_device(): lax.all_to_all(send_c, 'expert', split_axis=0, concat_axis=0, tiled=True)  62.4 us
    all_to_all x1, blocking collectives, on_device(): lax.all_to_all(send_x, 'expert', split_axis=0, concat_axis=0, tiled=True)  61.8 us
    all_gather x1, waiting for transfers between devices, on_device(): lax.all_gather(recv_x, 'dp', axis=0, tiled=True)  52.1 us
    all_to_all x1, waiting for transfers between devices, on_device(): lax.all_to_all(outgoing, 'expert', split_axis=0, concat_axis=0, tiled=True)  48 us
    dot_general x1, matrix products, expert_terms(): lax.dot_general(rows_x, pre_grad, (((0,), (0,)), ((), ())), preferred_ele...  14.3 us
    all_to_all x1, starting transfers between devices, on_device(): lax.all_to_all(outgoing, 'expert', split_axis=0, concat_axis=0, tiled=True)  10.5 us
  transfers between devices with their start and end apart: 3, of which 3 were waited for; matrix products, arithmetic and copies ran while one was open for 4% of the time, Pallas kernels for 0%

commit v1 on v0

--- a/solution.py
+++ b/solution.py
@@ -6,6 +6,13 @@
 BETA_ONE = 0.9
 BETA_TWO = 0.95
 EPSILON = 1e-08
+
+
+def gather_over(array, axis, along):
+    count = lax.axis_size(axis)
+    blocks = jnp.stack([array for _ in range(count)])
+    blocks = lax.all_to_all(blocks, axis, split_axis=0, concat_axis=0)
+    return jnp.concatenate(blocks, axis=along)
 
 
 def expert_terms(rows_x, rows_c, up_tile, down_tile):
@@ -73,7 +80,7 @@
     recv_c = recv_c.reshape(experts * capacity, model_width)
     grad_up, grad_cols = expert_terms(
         lax.all_gather(recv_x, "dp", axis=0, tiled=True),
-        lax.all_gather(recv_c, "dp", axis=0, tiled=True),
+        gather_over(recv_c, "dp", 0),
         w_up[0],
         w_down[0],
     )

time: 403 us -> 494 us (1.23)
  the two profiles are of different devices: /device:TPU:33 before, /device:TPU:1 now
where the time goes in v1:
time: 494 us; the launch traced here: 493 us
  waiting for transfers between devices  341 us (69%)
  starting transfers between devices  74.4 us (15%)
  matrix products  28.8 us (6%)
  local copies, waits for them, and re-layouts  25.7 us (5%)
  between operations  14.9 us (3%)
  other arithmetic  7.97 us (2%)
    all_gather x1, waiting for transfers between devices, on_device(): lax.all_gather(recv_x, 'dp', axis=0, tiled=True)  147 us
    all_to_all x1, waiting for transfers between devices, gather_over(): blocks = lax.all_to_all(blocks, axis, split_axis=0, concat_axis=0)  99.8 us
    all_to_all x1, starting transfers between devices, gather_over(): blocks = lax.all_to_all(blocks, axis, split_axis=0, concat_axis=0)  47.7 us
    all_to_all x1, waiting for transfers between devices, on_device(): lax.all_to_all(outgoing, 'expert', split_axis=0, concat_axis=0, tiled=True)  44.2 us
    all_to_all x1, waiting for transfers between devices, on_device(): lax.all_to_all(send_x, 'expert', split_axis=0, concat_axis=0, tiled=True)  31.6 us
    all_to_all x1, waiting for transfers between devices, on_device(): lax.all_to_all(send_c, 'expert', split_axis=0, concat_axis=0, tiled=True)  19.1 us
    all_to_all x1, starting transfers between devices, on_device(): lax.all_to_all(send_x, 'expert', split_axis=0, concat_axis=0, tiled=True)  14.5 us
    dot_general x1, matrix products, expert_terms(): lax.dot_general(rows_x, pre_grad, (((0,), (0,)), ((), ())), preferred_ele...  14.3 us
  transfers between devices with their start and end apart: 5, of which 5 were waited for; matrix products, arithmetic and copies ran while one was open for 5% of the time, Pallas kernels for 0%

profile of v1, /device:TPU:1, one launch (start us, length us, event | category | flops | bytes accessed | tf_op | source)
XLA Modules:
  0.0 493.3 jit_solution(416708973883627467)
XLA Ops:
  7.2 0.0 copy-start
  7.2 0.0 copy-start.8
  7.2 0.9 fusion.19
  8.1 0.2 reduce_window_sum.11
  8.2 0.8 select_reduce_fusion
  9.1 0.7 multiply_add_fusion
  9.7 1.4 multiply_convert_fusion
  11.1 0.0 copy-done.8
  11.1 0.7 convolution_convert_fusion
  11.9 1.2 fusion.25
  13.1 1.5 reshape.63
  14.6 14.5 %all-to-all-start = ((bf16[32,5,3584]{2,1,0:T(8,128)(2,1)}), bf16[32,5,3584]{2,1,0:T(8,128)(2,1)S(1)}, u32[]{:S(2)}, u32[]{:S(2)}) async-start(bf16[32,5,3584]{2,1,0:T(8,128)(2,1)} %reshape.63), calls=%async_computation | async-start | bytes 3670016 | tf_op jit(solution)/shard_map/all_to_all | solution.py:76
  29.1 2.5 reshape.65
  31.6 31.6 %all-to-all-done = bf16[32,5,3584]{2,1,0:T(8,128)(2,1)S(1)} async-done(((bf16[32,5,3584]{2,1,0:T(8,128)(2,1)}), bf16[32,5,3584]{2,1,0:T(8,128)(2,1)S(1)}, u32[]{:S(2)}, u32[]{:S(2)}) %all-to-all-start) | async-done | bytes 1146912 | tf_op jit(solution)/shard_map/all_to_all | solution.py:76
  63.2 1.3 copy-done.1
  64.4 4.0 all-to-all-start.1
  68.4 0.0 all-gather.2.cloned.1.call-start
  68.5 2.5 reshape.64
  71.0 0.0 all-gather.2.cloned.1.call-update
  71.0 19.1 %all-to-all-done.1 = bf16[32,5,3584]{2,1,0:T(8,128)(2,1)S(1)} async-done(((bf16[32,5,3584]{2,1,0:T(8,128)(2,1)}), bf16[32,5,3584]{2,1,0:T(8,128)(2,1)S(1)}, u32[]{:S(2)}, u32[]{:S(2)}) %all-to-all-start.1) | async-done | bytes 1146912 | tf_op jit(solution)/shard_map/all_to_all | solution.py:77
  90.1 1.3 stack_reshape.2
  91.3 5.6 %stack.3 = bf16[8,160,3584]{2,1,0:T(8,128)(2,1)} broadcast(bf16[160,3584]{1,0:T(8,128)(2,1)} %stack_reshape.2), dimensions={1,2} | broadcast | bytes 10321920 | tf_op jit(solution)/shard_map/stack | solution.py:13
  97.0 47.7 %all-to-all-start.2 = ((bf16[8,160,3584]{2,1,0:T(8,128)(2,1)}), bf16[8,160,3584]{2,1,0:T(8,128)(2,1)}, u32[]{:S(2)}, u32[]{:S(2)}) async-start(bf16[8,160,3584]{2,1,0:T(8,128)(2,1)} %stack.3), calls=%async_computation.2 | async-start | bytes 18350080 | tf_op jit(solution)/shard_map/all_to_all | solution.py:14
  145.4 0.0 copy-done.3
  145.4 0.0 copy-start.10
  145.4 1.3 copy.24
  146.7 0.0 copy-done.4
  146.7 1.3 copy.25
  148.0 0.0 copy-done.10
  148.0 0.1 select_reduce_fusion.1
  148.1 146.8 %all-gather.2.cloned.1.call-done = bf16[1280,3584]{1,0:T(8,128)(2,1)} async-done(((bf16[160,3584]{1,0:T(8,128)(2,1)}), bf16[1280,3584]{1,0:T(8,128)(2,1)}) %all-gather.2.cloned.1.call-update) | async-done | bytes 9175056 | tf_op jit(solution)/shard_map/all_gather | solution.py:82
  294.9 0.0 copy-done.9
  294.9 6.2 %fusion.14 = f32[1280,128]{1,0:T(8,128)S(1)} fusion(bf16[1280,3584]{1,0:T(8,128)(2,1)} %all-gather.2.cloned.1.call-done, bf16[1,3584,128]{2,1,0:T(8,128)(2,1)S(1)} %copy-done.9), kind=kOutput, calls=%fused_computation.24 | convolution fusion | flops 1174405120 | bytes 10747904 | tf_op jit(solution)/shard_map/dot_general | solution.py:19
  301.1 99.8 %all-to-all-done.2 = bf16[8,160,3584]{2,1,0:T(8,128)(2,1)} async-done(((bf16[8,160,3584]{2,1,0:T(8,128)(2,1)}), bf16[8,160,3584]{2,1,0:T(8,128)(2,1)}, u32[]{:S(2)}, u32[]{:S(2)}) %all-to-all-start.2) | async-done | bytes 9175072 | tf_op jit(solution)/shard_map/all_to_all | solution.py:14
  400.9 7.6 %fusion.12 = bf16[128,3584]{1,0:T(8,128)(2,1)} fusion(bf16[1,128,3584]{2,1,0:T(8,128)(2,1)} %param.21, bf16[1,128,3584]{2,1,0:T(8,128)(2,1)} %param.20, bf16[1280,3584]{1,0:T(8,128)(2,1)} %bitcast.4, f32[1280,128]{1,0:T(8,128)S(1)} %fusion.14), kind=kOutput, calls=%fused_computation.21 | convolution fusion | flops 1180729344 | bytes 12582912 | tf_op jit(solution)/shard_map/dot_general | solution.py:30
  408.5 0.0 copy-done
  408.5 0.0 copy-done.6
  408.5 14.3 %select_bitcast_fusion.1 = (bf16[1,3584,128]{1,2,0:T(8,128)(2,1)}, bf16[3584,128]{0,1:T(8,128)(2,1)}) fusion(pred[]{:T(512)S(6)} %ne.3, bf16[1,3584,128]{1,2,0:T(8,128)(2,1)S(1)} %copy-done.7, bf16[1,3584,128]{1,2,0:T(8,128)(2,1)S(1)} %copy-done.6, bf16[1280,3584]{1,0:T(8,128)(2,1)} %all-gather.2.cloned.1.call-done, bf16[1280,3584]{1,0:T(8,128)(2,1)} %bitcast.4, ...), kind=kOutput, calls=%fused_computation.28 | convolution fusion | flops 2356248576 | bytes 23592960 | tf_op jit(solution)/shard_map/dot_general | solution.py:27
  422.8 1.6 pad_maximum_fusion
  424.4 2.3 copy.26
  426.7 2.2 gather_fusion
  428.9 1.4 broadcast_select_fusion
  430.2 8.3 %all-to-all-start.3 = ((bf16[32,112,256]{2,1,0:T(8,128)(2,1)}), bf16[32,112,256]{2,1,0:T(8,128)(2,1)}, u32[]{:S(2)}, u32[]{:S(2)}) async-start(bf16[32,112,256]{2,1,0:T(8,128)(2,1)} %broadcast_select_fusion), calls=%async_computation.3 | async-start | bytes 3670016 | tf_op jit(solution)/shard_map/all_to_all | solution.py:95
  438.5 1.3 copy.27
  439.8 1.0 select_bitcast_fusion
  440.8 44.2 %all-to-all-done.3 = bf16[32,112,256]{2,1,0:T(8,128)(2,1)} async-done(((bf16[32,112,256]{2,1,0:T(8,128)(2,1)}), bf16[32,112,256]{2,1,0:T(8,128)(2,1)}, u32[]{:S(2)}, u32[]{:S(2)}) %all-to-all-start.3) | async-done | bytes 1835040 | tf_op jit(solution)/shard_map/all_to_all | solution.py:95
  485.0 0.8 dynamic-slice_bitcast_fusion
  485.8 0.6 slice_bitcast_fusion
  (13 shorter events, 0.0 us)
Async XLA Ops:
  7.2 401.4 %copy-start = (bf16[1,128,3584]{2,1,0:T(8,128)(2,1)S(1)}, bf16[1,128,3584]{2,1,0:T(8,128)(2,1)}, u32[]{:S(2)}) copy-start(bf16[1,128,3584]{2,1,0:T(8,128)(2,1)} %param.17) | copy-start | bytes 2752516
  7.2 4.0 copy-start.8
  14.6 48.6 %all-to-all-start = ((bf16[32,5,3584]{2,1,0:T(8,128)(2,1)}), bf16[32,5,3584]{2,1,0:T(8,128)(2,1)S(1)}, u32[]{:S(2)}, u32[]{:S(2)}) async-start(bf16[32,5,3584]{2,1,0:T(8,128)(2,1)} %reshape.63), calls=%async_computation | async-start | bytes 3670016 | tf_op jit(solution)/shard_map/all_to_all | solution.py:76
  63.2 1.3 copy-start.1
  64.4 25.6 %all-to-all-start.1 = ((bf16[32,5,3584]{2,1,0:T(8,128)(2,1)}), bf16[32,5,3584]{2,1,0:T(8,128)(2,1)S(1)}, u32[]{:S(2)}, u32[]{:S(2)}) async-start(bf16[32,5,3584]{2,1,0:T(8,128)(2,1)} %reshape.65), calls=%async_computation.1 | async-start | bytes 3670016 | tf_op jit(solution)/shard_map/all_to_all | solution.py:77
  68.4 226.5 %all-gather.2.cloned.1.call-start = ((), (), s32[]{:S(2)}) async-start(), calls=%async_computation.4 | async-start | bytes 10321920 | tf_op jit(solution)/shard_map/all_gather | solution.py:82
  97.0 48.4 %copy-start.3 = (bf16[1,3584,128]{2,1,0:T(8,128)(2,1)S(1)}, bf16[1,3584,128]{2,1,0:T(8,128)(2,1)}, u32[]{:S(2)}) copy-start(bf16[1,3584,128]{2,1,0:T(8,128)(2,1)} %param.18) | copy-start | bytes 2752516
  97.0 304.0 %all-to-all-start.2 = ((bf16[8,160,3584]{2,1,0:T(8,128)(2,1)}), bf16[8,160,3584]{2,1,0:T(8,128)(2,1)}, u32[]{:S(2)}, u32[]{:S(2)}) async-start(bf16[8,160,3584]{2,1,0:T(8,128)(2,1)} %stack.3), calls=%async_computation.2 | async-start | bytes 18350080 | tf_op jit(solution)/shard_map/all_to_all | solution.py:14
  144.7 2.0 copy-start.4
  145.4 2.6 copy-start.10
  146.7 148.2 %copy-start.9 = (bf16[1,3584,128]{2,1,0:T(8,128)(2,1)S(1)}, bf16[1,3584,128]{2,1,0:T(8,128)(2,1)}, u32[]{:S(2)}) copy-start(bf16[1,3584,128]{2,1,0:T(8,128)(2,1)} %param.16) | copy-start | bytes 2752516
  400.9 7.6 %copy-start.6 = (bf16[1,3584,128]{1,2,0:T(8,128)(2,1)S(1)}, bf16[1,3584,128]{1,2,0:T(8,128)(2,1)}, u32[]{:S(2)}) copy-start(bf16[1,3584,128]{1,2,0:T(8,128)(2,1)} %copy.24) | copy-start | bytes 2752516
  400.9 7.6 %copy-start.7 = (bf16[1,3584,128]{1,2,0:T(8,128)(2,1)S(1)}, bf16[1,3584,128]{1,2,0:T(8,128)(2,1)}, u32[]{:S(2)}) copy-start(bf16[1,3584,128]{1,2,0:T(8,128)(2,1)} %copy.25) | copy-start | bytes 2752516
  430.2 8.3 %copy-start.5 = (bf16[1,3584,128]{1,2,0:T(8,128)(2,1)S(1)}, bf16[1,3584,128]{1,2,0:T(8,128)(2,1)}, u32[]{:S(2)}) copy-start(bf16[1,3584,128]{1,2,0:T(8,128)(2,1)} %get-tuple-element.16) | copy-start | bytes 2752516
  430.2 54.7 %all-to-all-start.3 = ((bf16[32,112,256]{2,1,0:T(8,128)(2,1)}), bf16[32,112,256]{2,1,0:T(8,128)(2,1)}, u32[]{:S(2)}, u32[]{:S(2)}) async-start(bf16[32,112,256]{2,1,0:T(8,128)(2,1)} %broadcast_select_fusion), calls=%async_computation.3 | async-start | bytes 3670016 | tf_op jit(solution)/shard_map/all_to_all | solution.py:95
  438.5 1.3 copy-start.2
Sparse Core Ops, SparseCore 0:
  71.1 223.7 all-gather.1
